TPU v7x, 8 devices: a whole 2x2x1 slice. The times are simulated.
8 devices in a mesh: dp: 2 (over z, y), tp: 4 (over x, core).
Axes of the slice: x: 2, y: 2, z: 1, core: 2. Of those that a mesh axis runs over, the one named last changes fastest.
Arguments:
- x: bfloat16 [32, 8, 1280], P('dp'), parts along dimension 0
- w_in: bfloat16 [1280, 4, 2560], P(None, None, 'tp')
- w_deep: bfloat16 [3, 640, 4, 2560], P(None, None, None, 'tp')
- w_rec: bfloat16 [4, 640, 4, 2560], P(None, None, None, 'tp')
- bias: float32 [4, 4, 2560], P(None, None, 'tp')
- w_proj: bfloat16 [4, 2560, 640], P(None, 'tp')
- r_init: bfloat16 [4, 32, 640], P(None, 'dp', 'tp'), parts along dimension 1
- c_init: float32 [4, 32, 2560], P(None, 'dp', 'tp'), parts along dimension 1
Outputs:
- output 1: bfloat16 [32, 8, 640], P('dp', None, 'tp'), parts along dimension 0
- output 2: bfloat16 [4, 32, 640], P(None, 'dp', 'tp'), parts along dimension 1
- output 3: float32 [4, 32, 2560], P(None, 'dp', 'tp'), parts along dimension 1
There are 2 independent parts. A program takes and returns all parts, laid end to end along the dimension named above; an argument that names none is the same for every part.
All inputs are finite; a program needn't handle non-finite values.
Results may differ from a plain program's by a relative error of at most 0.00819144.
Values are sent between devices in bfloat16 or wider.
A program may use at most 1 GiB of HBM per device.

v0:
```python
import jax
import jax.numpy as jnp
from jax import lax
from jax.sharding import PartitionSpec as P


def cell_update(gate_x, r_full, c_prev, w_hh, bias_l, w_p):
    gates = gate_x + jnp.einsum('bp,pgh->bgh', r_full, w_hh, preferred_element_type=jnp.float32) + bias_l
    in_gate = jax.nn.sigmoid(gates[:, 0])
    forget_gate = jax.nn.sigmoid(gates[:, 1])
    out_gate = jax.nn.sigmoid(gates[:, 2])
    c_new = forget_gate * c_prev + in_gate * jnp.tanh(gates[:, 3])
    h_new = (out_gate * jnp.tanh(c_new)).astype(jnp.bfloat16)
    part_proj = jnp.dot(h_new, w_p, preferred_element_type=jnp.float32)
    return part_proj, c_new


def solution(mesh):
    def local_forward(x, w_in, w_deep, w_rec, bias, w_proj, r_init, c_init):
        num_layers = w_rec.shape[0]
        proj_local = r_init.shape[-1]
        shard_idx = lax.axis_index('tp')
        gate_in = jnp.einsum('btd,dgh->tbgh', x, w_in, preferred_element_type=jnp.float32)
        r_seq = None
        r_last_list = []
        c_last_list = []
        for layer in range(num_layers):
            if layer > 0:
                gate_in = jnp.einsum('tbp,pgh->tbgh', r_seq, w_deep[layer - 1], preferred_element_type=jnp.float32)
            w_hh = w_rec[layer]
            bias_l = bias[layer]
            w_p = w_proj[layer]
            r_start = lax.all_gather(r_init[layer], 'tp', axis=1, tiled=True)

            def step(carry, gate_t):
                r_full, r_piece, c_prev = carry
                part_proj, c_new = cell_update(gate_t, r_full, c_prev, w_hh, bias_l, w_p)
                piece_new = lax.psum_scatter(part_proj, 'tp', scatter_dimension=1, tiled=True).astype(jnp.bfloat16)
                full_new = lax.all_gather(piece_new, 'tp', axis=1, tiled=True)
                return (full_new, piece_new, c_new), full_new

            (r_full_end, r_piece_end, c_end), r_seq = lax.scan(step, (r_start, r_init[layer], c_init[layer]), gate_in)
            r_last_list.append(r_piece_end)
            c_last_list.append(c_end)
        y_local = lax.dynamic_slice_in_dim(r_seq, shard_idx * proj_local, proj_local, axis=2)
        y_local = jnp.swapaxes(y_local, 0, 1)
        return y_local, jnp.stack(r_last_list), jnp.stack(c_last_list)

    specs_in = (P('dp', None, None), P(None, None, 'tp'), P(None, None, None, 'tp'), P(None, None, None, 'tp'), P(None, None, 'tp'), P(None, 'tp', None), P(None, 'dp', 'tp'), P(None, 'dp', 'tp'))
    specs_out = (P('dp', None, 'tp'), P(None, 'dp', 'tp'), P(None, 'dp', 'tp'))
    return jax.shard_map(local_forward, mesh=mesh, in_specs=specs_in, out_specs=specs_out, check_vma=False)
```

profile of v0, /device:TPU:0, one launch (start us, length us, event | category | flops | bytes accessed | tf_op | source)
XLA Modules:
  0.0 988.9 jit_solution(14517990364367737508)
XLA Ops:
  40.2 220.6 %while.64 = (s32[]{:T(128)}, bf16[16,640]{1,0:T(8,128)(2,1)S(1)}, bf16[16,160]{1,0:T(8,128)(2,1)}, f32[16,640]{1,0:T(8,128)S(1)}, bf16[8,16,640]{2,1,0:T(8,128)(...) while((s32[]{:T(128)}, bf16[16,640]{1,0:T(8,128)(2,1)S(1)}, ...), condition=%wide.region_2.3_spmd, body=%wide.region_0.2_spmd.sunk | while | flops 65761280 | bytes 8755413 | solution.py:42
  69.8 16.4 %reduce-scatter.21.cloned.1.call-done = f32[160,16]{1,0:T(8,128)} async-done(((f32[640,16]{1,0:T(8,128)}), f32[160,16]{1,0:T(8,128)}) %reduce-scatter.21.cloned.1.call-update) | async-done | bytes 10256 | tf_op jit(solution)/shard_map/while
  97.7 16.3 %reduce-scatter.21.cloned.1.call-done = f32[160,16]{1,0:T(8,128)} async-done(((f32[640,16]{1,0:T(8,128)}), f32[160,16]{1,0:T(8,128)}) %reduce-scatter.21.cloned.1.call-update) | async-done | bytes 10256 | tf_op jit(solution)/shard_map/while
  125.5 16.0 %reduce-scatter.21.cloned.1.call-done = f32[160,16]{1,0:T(8,128)} async-done(((f32[640,16]{1,0:T(8,128)}), f32[160,16]{1,0:T(8,128)}) %reduce-scatter.21.cloned.1.call-update) | async-done | bytes 10256 | tf_op jit(solution)/shard_map/while
  180.6 16.0 %reduce-scatter.21.cloned.1.call-done = f32[160,16]{1,0:T(8,128)} async-done(((f32[640,16]{1,0:T(8,128)}), f32[160,16]{1,0:T(8,128)}) %reduce-scatter.21.cloned.1.call-update) | async-done | bytes 10256 | tf_op jit(solution)/shard_map/while
  208.1 16.3 %reduce-scatter.21.cloned.1.call-done = f32[160,16]{1,0:T(8,128)} async-done(((f32[640,16]{1,0:T(8,128)}), f32[160,16]{1,0:T(8,128)}) %reduce-scatter.21.cloned.1.call-update) | async-done | bytes 10256 | tf_op jit(solution)/shard_map/while
  235.9 16.3 %reduce-scatter.21.cloned.1.call-done = f32[160,16]{1,0:T(8,128)} async-done(((f32[640,16]{1,0:T(8,128)}), f32[160,16]{1,0:T(8,128)}) %reduce-scatter.21.cloned.1.call-update) | async-done | bytes 10256 | tf_op jit(solution)/shard_map/while
  284.4 220.1 %while.65 = (s32[]{:T(128)}, bf16[16,640]{1,0:T(8,128)(2,1)S(1)}, bf16[16,160]{1,0:T(8,128)(2,1)}, f32[16,640]{1,0:T(8,128)S(1)}, bf16[8,16,640]{2,1,0:T(8,128)(...) while((s32[]{:T(128)}, bf16[16,640]{1,0:T(8,128)(2,1)S(1)}, ...), condition=%wide.region_5.6_spmd, body=%wide.region_3.5_spmd.sunk | while | flops 65761280 | bytes 8755413 | solution.py:42
  341.5 16.3 %reduce-scatter.23.cloned.1.call-done = f32[160,16]{1,0:T(8,128)} async-done(((f32[640,16]{1,0:T(8,128)}), f32[160,16]{1,0:T(8,128)}) %reduce-scatter.23.cloned.1.call-update) | async-done | bytes 10256 | tf_op jit(solution)/shard_map/while
  396.9 16.3 %reduce-scatter.23.cloned.1.call-done = f32[160,16]{1,0:T(8,128)} async-done(((f32[640,16]{1,0:T(8,128)}), f32[160,16]{1,0:T(8,128)}) %reduce-scatter.23.cloned.1.call-update) | async-done | bytes 10256 | tf_op jit(solution)/shard_map/while
  424.7 16.0 %reduce-scatter.23.cloned.1.call-done = f32[160,16]{1,0:T(8,128)} async-done(((f32[640,16]{1,0:T(8,128)}), f32[160,16]{1,0:T(8,128)}) %reduce-scatter.23.cloned.1.call-update) | async-done | bytes 10256 | tf_op jit(solution)/shard_map/while
  521.1 220.4 %while.66 = (s32[]{:T(128)}, bf16[16,640]{1,0:T(8,128)(2,1)S(1)}, bf16[16,160]{1,0:T(8,128)(2,1)}, f32[16,640]{1,0:T(8,128)S(1)}, bf16[8,16,640]{2,1,0:T(8,128)(...) while((s32[]{:T(128)}, bf16[16,640]{1,0:T(8,128)(2,1)S(1)}, ...), condition=%wide.region_8.9_spmd, body=%wide.region_6.8_spmd.sunk | while | flops 65761280 | bytes 8755413 | solution.py:42
  550.4 16.0 %reduce-scatter.25.cloned.1.call-done = f32[160,16]{1,0:T(8,128)} async-done(((f32[640,16]{1,0:T(8,128)}), f32[160,16]{1,0:T(8,128)}) %reduce-scatter.25.cloned.1.call-update) | async-done | bytes 10256 | tf_op jit(solution)/shard_map/while
  578.0 16.3 %reduce-scatter.25.cloned.1.call-done = f32[160,16]{1,0:T(8,128)} async-done(((f32[640,16]{1,0:T(8,128)}), f32[160,16]{1,0:T(8,128)}) %reduce-scatter.25.cloned.1.call-update) | async-done | bytes 10256 | tf_op jit(solution)/shard_map/while
  633.3 16.3 %reduce-scatter.25.cloned.1.call-done = f32[160,16]{1,0:T(8,128)} async-done(((f32[640,16]{1,0:T(8,128)}), f32[160,16]{1,0:T(8,128)}) %reduce-scatter.25.cloned.1.call-update) | async-done | bytes 10256 | tf_op jit(solution)/shard_map/while
  661.2 16.3 %reduce-scatter.25.cloned.1.call-done = f32[160,16]{1,0:T(8,128)} async-done(((f32[640,16]{1,0:T(8,128)}), f32[160,16]{1,0:T(8,128)}) %reduce-scatter.25.cloned.1.call-update) | async-done | bytes 10256 | tf_op jit(solution)/shard_map/while
  689.0 16.3 %reduce-scatter.25.cloned.1.call-done = f32[160,16]{1,0:T(8,128)} async-done(((f32[640,16]{1,0:T(8,128)}), f32[160,16]{1,0:T(8,128)}) %reduce-scatter.25.cloned.1.call-update) | async-done | bytes 10256 | tf_op jit(solution)/shard_map/while
  758.1 220.7 %while.67 = (s32[]{:T(128)}, bf16[16,640]{1,0:T(8,128)(2,1)S(1)}, bf16[16,160]{1,0:T(8,128)(2,1)}, f32[16,640]{1,0:T(8,128)S(1)}, bf16[8,16,640]{2,1,0:T(8,128)(...) while((s32[]{:T(128)}, bf16[16,640]{1,0:T(8,128)(2,1)S(1)}, ...), condition=%wide.region_11.12_spmd, body=%wide.region_9.11_spmd.sunk | while | flops 65761280 | bytes 8755413 | solution.py:42
  787.7 16.0 %reduce-scatter.27.cloned.1.call-done = f32[160,16]{1,0:T(8,128)} async-done(((f32[640,16]{1,0:T(8,128)}), f32[160,16]{1,0:T(8,128)}) %reduce-scatter.27.cloned.1.call-update) | async-done | bytes 10256 | tf_op jit(solution)/shard_map/while
  842.7 16.4 %reduce-scatter.27.cloned.1.call-done = f32[160,16]{1,0:T(8,128)} async-done(((f32[640,16]{1,0:T(8,128)}), f32[160,16]{1,0:T(8,128)}) %reduce-scatter.27.cloned.1.call-update) | async-done | bytes 10256 | tf_op jit(solution)/shard_map/while
  870.6 16.3 %reduce-scatter.27.cloned.1.call-done = f32[160,16]{1,0:T(8,128)} async-done(((f32[640,16]{1,0:T(8,128)}), f32[160,16]{1,0:T(8,128)}) %reduce-scatter.27.cloned.1.call-update) | async-done | bytes 10256 | tf_op jit(solution)/shard_map/while
  898.4 16.0 %reduce-scatter.27.cloned.1.call-done = f32[160,16]{1,0:T(8,128)} async-done(((f32[640,16]{1,0:T(8,128)}), f32[160,16]{1,0:T(8,128)}) %reduce-scatter.27.cloned.1.call-update) | async-done | bytes 10256 | tf_op jit(solution)/shard_map/while
  925.9 16.3 %reduce-scatter.27.cloned.1.call-done = f32[160,16]{1,0:T(8,128)} async-done(((f32[640,16]{1,0:T(8,128)}), f32[160,16]{1,0:T(8,128)}) %reduce-scatter.27.cloned.1.call-update) | async-done | bytes 10256 | tf_op jit(solution)/shard_map/while
  953.7 16.3 %reduce-scatter.27.cloned.1.call-done = f32[160,16]{1,0:T(8,128)} async-done(((f32[640,16]{1,0:T(8,128)}), f32[160,16]{1,0:T(8,128)}) %reduce-scatter.27.cloned.1.call-update) | async-done | bytes 10256 | tf_op jit(solution)/shard_map/while
  (518 shorter events, 649.2 us)
Async XLA Ops:
  67.0 19.2 %reduce-scatter.21.cloned.1.call-start = ((), (), s32[]{:S(2)}) async-start(), calls=%async_computation.4 | async-start | bytes 409600 | tf_op jit(solution)/shard_map/while
  94.9 19.1 %reduce-scatter.21.cloned.1.call-start = ((), (), s32[]{:S(2)}) async-start(), calls=%async_computation.4 | async-start | bytes 409600 | tf_op jit(solution)/shard_map/while
  122.7 18.9 %reduce-scatter.21.cloned.1.call-start = ((), (), s32[]{:S(2)}) async-start(), calls=%async_computation.4 | async-start | bytes 409600 | tf_op jit(solution)/shard_map/while
  205.3 19.1 %reduce-scatter.21.cloned.1.call-start = ((), (), s32[]{:S(2)}) async-start(), calls=%async_computation.4 | async-start | bytes 409600 | tf_op jit(solution)/shard_map/while
  233.1 19.1 %reduce-scatter.21.cloned.1.call-start = ((), (), s32[]{:S(2)}) async-start(), calls=%async_computation.4 | async-start | bytes 409600 | tf_op jit(solution)/shard_map/while
  311.1 18.8 %reduce-scatter.23.cloned.1.call-start = ((), (), s32[]{:S(2)}) async-start(), calls=%async_computation.5 | async-start | bytes 409600 | tf_op jit(solution)/shard_map/while
  338.7 19.1 %reduce-scatter.23.cloned.1.call-start = ((), (), s32[]{:S(2)}) async-start(), calls=%async_computation.5 | async-start | bytes 409600 | tf_op jit(solution)/shard_map/while
  394.0 19.1 %reduce-scatter.23.cloned.1.call-start = ((), (), s32[]{:S(2)}) async-start(), calls=%async_computation.5 | async-start | bytes 409600 | tf_op jit(solution)/shard_map/while
  421.9 18.8 %reduce-scatter.23.cloned.1.call-start = ((), (), s32[]{:S(2)}) async-start(), calls=%async_computation.5 | async-start | bytes 409600 | tf_op jit(solution)/shard_map/while
  449.4 18.8 %reduce-scatter.23.cloned.1.call-start = ((), (), s32[]{:S(2)}) async-start(), calls=%async_computation.5 | async-start | bytes 409600 | tf_op jit(solution)/shard_map/while
  476.9 18.8 %reduce-scatter.23.cloned.1.call-start = ((), (), s32[]{:S(2)}) async-start(), calls=%async_computation.5 | async-start | bytes 409600 | tf_op jit(solution)/shard_map/while
  547.6 18.9 %reduce-scatter.25.cloned.1.call-start = ((), (), s32[]{:S(2)}) async-start(), calls=%async_computation.6 | async-start | bytes 409600 | tf_op jit(solution)/shard_map/while
  575.1 19.2 %reduce-scatter.25.cloned.1.call-start = ((), (), s32[]{:S(2)}) async-start(), calls=%async_computation.6 | async-start | bytes 409600 | tf_op jit(solution)/shard_map/while
  603.0 18.8 %reduce-scatter.25.cloned.1.call-start = ((), (), s32[]{:S(2)}) async-start(), calls=%async_computation.6 | async-start | bytes 409600 | tf_op jit(solution)/shard_map/while
  630.5 19.2 %reduce-scatter.25.cloned.1.call-start = ((), (), s32[]{:S(2)}) async-start(), calls=%async_computation.6 | async-start | bytes 409600 | tf_op jit(solution)/shard_map/while
  658.4 19.1 %reduce-scatter.25.cloned.1.call-start = ((), (), s32[]{:S(2)}) async-start(), calls=%async_computation.6 | async-start | bytes 409600 | tf_op jit(solution)/shard_map/while
  686.2 19.2 %reduce-scatter.25.cloned.1.call-start = ((), (), s32[]{:S(2)}) async-start(), calls=%async_computation.6 | async-start | bytes 409600 | tf_op jit(solution)/shard_map/while
  714.0 18.8 %reduce-scatter.25.cloned.1.call-start = ((), (), s32[]{:S(2)}) async-start(), calls=%async_computation.6 | async-start | bytes 409600 | tf_op jit(solution)/shard_map/while
  784.9 18.9 %reduce-scatter.27.cloned.1.call-start = ((), (), s32[]{:S(2)}) async-start(), calls=%async_computation.7 | async-start | bytes 409600 | tf_op jit(solution)/shard_map/while
  839.9 19.2 %reduce-scatter.27.cloned.1.call-start = ((), (), s32[]{:S(2)}) async-start(), calls=%async_computation.7 | async-start | bytes 409600 | tf_op jit(solution)/shard_map/while
  867.7 19.1 %reduce-scatter.27.cloned.1.call-start = ((), (), s32[]{:S(2)}) async-start(), calls=%async_computation.7 | async-start | bytes 409600 | tf_op jit(solution)/shard_map/while
  895.6 18.9 %reduce-scatter.27.cloned.1.call-start = ((), (), s32[]{:S(2)}) async-start(), calls=%async_computation.7 | async-start | bytes 409600 | tf_op jit(solution)/shard_map/while
  923.1 19.2 %reduce-scatter.27.cloned.1.call-start = ((), (), s32[]{:S(2)}) async-start(), calls=%async_computation.7 | async-start | bytes 409600 | tf_op jit(solution)/shard_map/while
  950.9 19.2 %reduce-scatter.27.cloned.1.call-start = ((), (), s32[]{:S(2)}) async-start(), calls=%async_computation.7 | async-start | bytes 409600 | tf_op jit(solution)/shard_map/while
  (84 other events, 1141.5 us)
Sparse Core Ops, SparseCore 0:
  70.2 15.9 reduce-scatter.20
  98.1 15.8 reduce-scatter.20
  125.6 15.8 reduce-scatter.20
  153.2 15.8 reduce-scatter.20
  180.7 15.8 reduce-scatter.20
  208.5 15.8 reduce-scatter.20
  236.3 15.8 reduce-scatter.20
  341.9 15.8 reduce-scatter.22
  397.3 15.8 reduce-scatter.22
  424.8 15.8 reduce-scatter.22
  452.4 15.8 reduce-scatter.22
  550.5 15.8 reduce-scatter.24
  578.4 15.8 reduce-scatter.24
  605.9 15.8 reduce-scatter.24
  633.8 15.8 reduce-scatter.24
  689.4 15.8 reduce-scatter.24
  717.0 15.8 reduce-scatter.24
  787.8 15.8 reduce-scatter.26
  815.3 15.8 reduce-scatter.26
  843.1 15.8 reduce-scatter.26
  871.0 15.8 reduce-scatter.26
  898.5 15.8 reduce-scatter.26
  926.3 15.8 reduce-scatter.26
  954.2 15.8 reduce-scatter.26
  (8 shorter events, 122.1 us)
where the time goes:
time: 992 us; the launch traced here: 989 us
  waiting for transfers between devices  514 us (52%)
  blocking collectives  264 us (27%)
  matrix products  98.9 us (10%)
  local copies, waits for them, and re-layouts  94 us (9%)
  between operations  13.8 us (1%)
    while x64, waiting for transfers between devices  514 us
    all_gather x32, blocking collectives, step(): full_new = lax.all_gather(piece_new, 'tp', axis=1, tiled=True)  224 us
    dot_general x32, matrix products, cell_update(): jnp.einsum('bp,pgh->bgh', r_full, w_hh, preferred_element_type=jnp.float32)  48.9 us
    all_gather x4, blocking collectives, local_forward(): r_start = lax.all_gather(r_init[layer], 'tp', axis=1, tiled=True)  39.5 us
    while x32, matrix products  38.6 us
    while x192, local copies, waits for them, and re-layouts  33.4 us
  transfers between devices with their start and end apart: 32, of which 32 were waited for; matrix products, arithmetic and copies ran while one was open for 0% of the time, Pallas kernels for 0%

commit v1 on v0

v1 whole, which is shorter than its diff:
```python
import functools

import jax
import jax.numpy as jnp
from jax import lax
from jax.experimental import pallas as pl
from jax.experimental.pallas import tpu as pltpu
from jax.sharding import PartitionSpec as P

MESH = pl.DeviceIdType.MESH
F32, BF16 = jnp.float32, jnp.bfloat16
L, T, B = 4, 8, 16
KX, KR, C = 1280, 640, 640
NB = C // 128
Q = 4 * NB
KC = 64
XC = 256
NX = KX // XC


def regroup(raw, row0, dst, dst0, scr, n):
    def chunk(j, carry):
        src = pl.multiple_of(row0 + j * (KC * Q), KC * Q)
        k0 = pl.multiple_of(dst0 + j * KC, KC)
        scr[...] = raw[pl.ds(src, KC * Q), :].astype(F32)
        for q in range(Q):
            dst[pl.ds(k0, KC), q * 128:(q + 1) * 128] = scr[pl.ds(q, KC, stride=Q), :].astype(BF16)
        return carry

    lax.fori_loop(0, n, chunk, 0)


def kernel(x_hbm, win_hbm, wdeep_hbm, wrec_hbm, bias_hbm, wproj_hbm, rinit_ref, cinit_hbm,
           y_ref, rlast_ref, c_ref,
           x_v, xraw, raw, w_v, wx, wp, bias_v, gx, scr, rbuf, rcur, yfull,
           part, csum, rx1, rx2,
           ld_sem, x_sem, w_sem, wp_sem, ri_send, ri_recv, s1, r1, s2, r2):
    dp = lax.axis_index("dp")
    me = lax.axis_index("tp")
    chip, core = me // 2, me % 2
    partner = chip * 2 + 1 - core
    other = (1 - chip) * 2

    def dev(tp):
        return (dp, tp)

    def load_w(m):
        src = wrec_hbm.at[m] if m < L else wdeep_hbm.at[m - L]
        return pltpu.make_async_copy(src.reshape(KR * Q, 128), raw.at[m], w_sem.at[m])

    def load_x(j):
        return pltpu.make_async_copy(
            win_hbm.reshape(KX * Q, 128).at[pl.ds(j * XC * Q, XC * Q)],
            xraw.at[pl.ds(j * XC * Q, XC * Q)], x_sem.at[j])

    def load_p(l):
        return pltpu.make_async_copy(wproj_hbm.at[l], wp.at[l], wp_sem.at[l])

    load_w(0).start()
    ld_x = pltpu.make_async_copy(x_hbm, x_v, ld_sem.at[0])
    ld_x.start()
    for j in range(NX):
        load_x(j).start()
    ld_b = pltpu.make_async_copy(bias_hbm, bias_v, ld_sem.at[1])
    ld_c = pltpu.make_async_copy(cinit_hbm, c_ref, ld_sem.at[2])
    ld_b.start()
    ld_c.start()
    load_p(0).start()

    peers = (partner, other, other + 1)
    barrier = pltpu.get_barrier_semaphore()
    for p in peers:
        pl.semaphore_signal(barrier, inc=1, device_id=dev(p), device_id_type=MESH)
    pl.semaphore_wait(barrier, 3)

    def piece(i, p):
        return pltpu.make_async_remote_copy(
            src_ref=rinit_ref, dst_ref=rbuf.at[me], send_sem=ri_send.at[i], recv_sem=ri_recv.at[me],
            device_id=dev(p), device_id_type=MESH)

    for i, p in enumerate(peers):
        piece(i, p).start()

    load_w(0).wait()
    regroup(raw.at[0], 0, w_v.at[0], 0, scr, KR // KC)
    ld_x.wait()
    gx[...] = jnp.zeros_like(gx)

    def x_chunk(j, carry):
        pltpu.make_async_copy(
            win_hbm.reshape(KX * Q, 128).at[pl.ds(j * XC * Q, XC * Q)],
            xraw.at[pl.ds(j * XC * Q, XC * Q)], x_sem.at[j]).wait()
        regroup(xraw, j * XC * Q, wx, 0, scr, XC // KC)
        xs = x_v[:, :, pl.ds(pl.multiple_of(j * XC, XC), XC)].reshape(B * T, XC)
        d = jnp.dot(xs, wx[...], preferred_element_type=F32)
        for q in range(Q):
            gx[q] += d[:, q * 128:(q + 1) * 128]
        return carry

    lax.fori_loop(0, NX, x_chunk, 0)

    order = (1, L, 2, L + 1, 3, L + 2)
    for m in order:
        load_w(m).start()
    for l in range(1, L):
        load_p(l).start()

    for i, p in enumerate(peers):
        piece(i, p).wait_send()
        pltpu.make_async_remote_copy(
            src_ref=rinit_ref, dst_ref=rbuf.at[p], send_sem=ri_send.at[i], recv_sem=ri_recv.at[p],
            device_id=dev(p), device_id_type=MESH).wait_recv()
    rbuf[me] = rinit_ref[...]
    for l in range(L):
        rcur[l] = jnp.concatenate([rbuf[j, l].astype(F32) for j in range(4)], axis=1).astype(BF16)
    ld_b.wait()
    ld_c.wait()

    def copy1(l, par):
        return pltpu.make_async_remote_copy(
            src_ref=part.at[l], dst_ref=rx1.at[l, par], send_sem=s1.at[l], recv_sem=r1.at[l, par],
            device_id=dev(partner), device_id_type=MESH)

    def copy2(l, par, j, rows):
        half = pl.ds(pl.multiple_of(rows * 8, 8), 8)
        return pltpu.make_async_remote_copy(
            src_ref=csum.at[l, half], dst_ref=rx2.at[l, par, half], send_sem=s2.at[l, j],
            recv_sem=r2.at[l, par, rows], device_id=dev(other + j), device_id_type=MESH)

    def node(l, t):
        @pl.when(t == 0)
        def _():
            load_p(l).wait()

        g = jnp.dot(rcur[l], w_v[l], preferred_element_type=F32)
        if l == 0:
            g = g + jnp.concatenate([gx[q, pl.ds(t, B, stride=T), :] for q in range(Q)], axis=1)
        else:
            g = g + jnp.dot(rcur[l - 1], w_v[L + l - 1], preferred_element_type=F32)
        h = []
        for cb in range(NB):
            cols = slice(cb * 128, (cb + 1) * 128)
            gate = [g[:, (cb * 4 + k) * 128:(cb * 4 + k + 1) * 128] + bias_v[l, k:k + 1, cols] for k in range(4)]
            c_new = jax.nn.sigmoid(gate[1]) * c_ref[l, :, cols] + jax.nn.sigmoid(gate[0]) * jnp.tanh(gate[3])
            c_ref[l, :, cols] = c_new
            h.append((jax.nn.sigmoid(gate[2]) * jnp.tanh(c_new)).astype(BF16))
        part[l] = jnp.dot(jnp.concatenate(h, axis=1), wp[l], preferred_element_type=F32)
        copy1(l, t % 2).start()

    def middle(l, t):
        par = t % 2
        copy1(l, par).wait_recv()
        csum[l] = part[l] + rx1[l, par]
        for j in range(2):
            copy2(l, par, j, core).start()

    def final(l, t):
        par = t % 2
        for rows in range(2):
            copy2(l, par, 0, rows).wait_recv()
        copy1(l, par).wait_send()
        for j in range(2):
            copy2(l, par, j, core).wait_send()
        r = (csum[l] + rx2[l, par]).astype(BF16)
        rcur[l] = r
        if l == L - 1:
            for q in range(KR // 128):
                yfull[q, pl.ds(t, B, stride=T), :] = r[:, q * 128:(q + 1) * 128].astype(F32)

    def regroup_w(m):
        load_w(m).wait()
        regroup(raw.at[m], 0, w_v.at[m], 0, scr, KR // KC)

    def round_(s, carry):
        def active(l, back):
            t = s - back - l
            return jnp.logical_and(t >= 0, t < T)

        for l in range(L):
            @pl.when(active(l, 1))
            def _():
                final(l, s - 1 - l)

            @pl.when(active(l, 0))
            def _():
                node(l, s - l)

            if l > 0:
                @pl.when(active(l - 1, 0))
                def _():
                    if l < L:
                        @pl.when(s == l - 1)
                        def _():
                            regroup_w(l)
                    middle(l - 1, s - l + 1)
            if l > 0:
                @pl.when(s == l - 1)
                def _():
                    regroup_w(L + l - 1)

        @pl.when(active(L - 1, 0))
        def _():
            middle(L - 1, s - L + 1)
        return carry

    lax.fori_loop(0, T + L, round_, 0)

    for j in range(4):
        @pl.when(me == j)
        def _():
            cols = slice(j * 160, (j + 1) * 160)
            y = jnp.concatenate([yfull[q] for q in range(KR // 128)], axis=1)[:, cols]
            y_ref[...] = y.reshape(B, T, 160).astype(BF16)
            rlast_ref[...] = rcur[:, :, cols]


def solution(mesh):
    def local(x, w_in, w_deep, w_rec, bias, w_proj, r_init, c_init):
        def split(w):
            w = w.reshape(w.shape[:-1] + (NB, 128))
            return jnp.swapaxes(w, -3, -2)

        any_ = pl.BlockSpec(memory_space=pl.ANY)
        vmem = pl.BlockSpec(memory_space=pltpu.VMEM)
        dma = pltpu.SemaphoreType.DMA
        return pl.pallas_call(
            kernel,
            out_shape=(jax.ShapeDtypeStruct((B, T, 160), BF16),
                       jax.ShapeDtypeStruct((L, B, 160), BF16),
                       jax.ShapeDtypeStruct((L, B, C), F32)),
            in_specs=[any_] * 6 + [vmem, any_],
            out_specs=(vmem, vmem, vmem),
            scratch_shapes=[
                pltpu.VMEM((B, T, KX), BF16),
                pltpu.VMEM((KX * Q, 128), BF16),
                pltpu.VMEM((2 * L - 1, KR * Q, 128), BF16),
                pltpu.VMEM((2 * L - 1, KR, 4 * C), BF16),
                pltpu.VMEM((XC, 4 * C), BF16),
                pltpu.VMEM((L, C, KR), BF16),
                pltpu.VMEM((L, 4, C), F32),
                pltpu.VMEM((Q, B * T, 128), F32),
                pltpu.VMEM((KC * Q, 128), F32),
                pltpu.VMEM((4, L, B, 160), BF16),
                pltpu.VMEM((L, B, KR), BF16),
                pltpu.VMEM((KR // 128, B * T, 128), F32),
                pltpu.VMEM((L, B, KR), F32),
                pltpu.VMEM((L, B, KR), F32),
                pltpu.VMEM((L, 2, B, KR), F32),
                pltpu.VMEM((L, 2, B, KR), F32),
                dma((3,)), dma((NX,)), dma((2 * L - 1,)), dma((L,)),
                dma((3,)), dma((4,)), dma((L,)), dma((L, 2)), dma((L, 2)), dma((L, 2, 2)),
            ],
            compiler_params=pltpu.CompilerParams(
                collective_id=0, has_side_effects=True, vmem_limit_bytes=66_000_000),
        )(x, split(w_in), split(w_deep), split(w_rec), bias, w_proj, r_init, c_init)

    specs_in = (P('dp', None, None), P(None, None, 'tp'), P(None, None, None, 'tp'), P(None, None, None, 'tp'),
                P(None, None, 'tp'), P(None, 'tp', None), P(None, 'dp', 'tp'), P(None, 'dp', 'tp'))
    specs_out = (P('dp', None, 'tp'), P(None, 'dp', 'tp'), P(None, 'dp', 'tp'))
    return jax.shard_map(local, mesh=mesh, in_specs=specs_in, out_specs=specs_out, check_vma=False)
```

time: 992 us -> 77.2 us (0.08)
  waiting for transfers between devices: 514 us -> 0 us
  blocking collectives: 264 us -> 0 us
  matrix products: 98.9 us -> 0 us
  local copies, waits for them, and re-layouts: 94 us -> 4.44 us
  Pallas kernels: 0 us -> 71.8 us
  between operations: 13.8 us -> 0.64 us
    while x64 -> x0, waiting for transfers between devices: 514 us -> none
    all_gather x36 -> x0, blocking collectives: 264 us -> none  [the longest x32 224 us: step(): full_new = lax.all_gather(piece_new, 'tp', axis=1, tiled=True)]
    pallas_call x0 -> x1, Pallas kernels: none -> 71.8 us  [local(): pl.pallas_call(kernel, out_shape=(jax.ShapeDtypeStruct((B, T, 160), BF16)...]
    dot_general x36 -> x0, matrix products: 60.3 us -> none  [the longest x32 48.9 us: cell_update(): jnp.einsum('bp,pgh->bgh', r_full, w_hh, preferred_element_type=jnp.float32)]
    while x32 -> x0, matrix products: 38.6 us -> none
    while x193 -> x0, local copies, waits for them, and re-layouts: 34.3 us -> none
    slice x7 -> x0, local copies, waits for them, and re-layouts: 21 us -> none  [the longest x1 11.5 us: local_forward(): w_hh = w_rec[layer]]
    dynamic_update_slice x32 -> x0, local copies, waits for them, and re-layouts: 19.6 us -> none  [local_forward(): lax.scan(step, (r_start, r_init[layer], c_init[layer]), gate_in)]
  transfers between devices with their start and end apart: 32 -> 0, of which waited for: 32 -> 0; matrix products, arithmetic and copies ran while one was open for 0% -> 0% of each run, Pallas kernels for 0% -> 0%
where the time goes in v1:
time: 77.2 us; the launch traced here: 76.9 us
  Pallas kernels  71.8 us (93%)
  local copies, waits for them, and re-layouts  4.44 us (6%)
    pallas_call x1, Pallas kernels, local(): pl.pallas_call(kernel, out_shape=(jax.ShapeDtypeStruct((B, T, 160), BF16)...  71.8 us
    unnamed x3, local copies, waits for them, and re-layouts  4.44 us

profile of v1, /device:TPU:0, one launch (start us, length us, event | category | flops | bytes accessed | tf_op | source)
XLA Modules:
  0.0 76.9 jit_solution(12271661067577052217)
XLA Ops:
  0.6 71.8 %shard_map.103 = (bf16[16,8,160]{2,1,0:T(8,128)(2,1)}, bf16[4,16,160]{2,1,0:T(8,128)(2,1)}, f32[4,16,640]{2,1,0:T(8,128)}) custom-call(bf16[16,8,1280]{2,1,0:T(8,128)(2,1)} %x_hbm.1, bf16[1280,5,4,128]{3,2,1,0:T(4,128)(2,1)} %bitcast.11, bf16[3,640,5,4,128]{4,3,2,1,0:T(4,128)(2,1)} %bitcast.10, bf16[4,640,5,4,128]{4,3,2,1,0:T(4,128)(2,1)} %bitcast.9, ...), custom_call_target="tpu_custom_call" | custom-call | tf_op jit(solution)/shard_map/pallas_call | solution.py:226
  72.5 1.5 %copy.14 = bf16[16,8,160]{2,1,0:T(8,128)(2,1)} copy(bf16[16,8,160]{2,1,0:T(8,128)(2,1)} %get-tuple-element.6) | data formatting | bytes 81920
  73.9 1.4 %copy.15 = bf16[4,16,160]{2,1,0:T(8,128)(2,1)} copy(bf16[4,16,160]{2,1,0:T(8,128)(2,1)} %get-tuple-element.7) | data formatting | bytes 40960
  75.3 1.6 %copy.16 = f32[4,16,640]{2,1,0:T(8,128)} copy(f32[4,16,640]{2,1,0:T(8,128)} %get-tuple-element.8) | data formatting | bytes 327680
